TPU v7x, 32 devices: a whole 2x2x4 slice. The times are simulated.
32 devices in a mesh: dp: 8 (over z, x), tensor: 4 (over y, core).
Axes of the slice: x: 2, y: 2, z: 4, core: 2. Of those that a mesh axis runs over, the one named last changes fastest.
Arguments:
- hidden_in: bfloat16 [32, 128, 4096], P(('dp', 'tensor')), parts along dimension 0, may hold values from -6 to 6
- norm_gain: float32 [4096], replicated, may hold values from 0.1 to 1.9
- query_weight: bfloat16 [4096, 4096], P(None, 'tensor'), may hold values from -3 to 3
- kv_weight: bfloat16 [4096, 2048], P(None, 'tensor'), may hold values from -3 to 3
- output_weight: bfloat16 [4096, 4096], P('tensor'), may hold values from -0.09375 to 0.09375
Outputs:
- attention_out: bfloat16 [32, 128, 4096], P(('dp', 'tensor')), parts along dimension 0
There are 8 independent parts, one for each index of `dp`. A program takes and returns all parts, laid end to end along the dimension named above; an argument that names none is the same for every part. Nothing has to cross between parts.
All inputs are finite; a program needn't handle non-finite values.
Results may differ from a plain program's by a relative error of at most 0.014.
The roundings to bfloat16 on the way count: a program that leaves them out, or rounds other values in their place, can miss the bound.
Values may be sent and summed in bfloat16 or wider, within the bound.
A program may use at most 128 MiB of HBM per device.

v0:
```python
import functools
import math

import jax
import jax.numpy as jnp
from jax import lax
import numpy as np
from jax.experimental import pallas as pl
from jax.experimental.pallas import tpu as pltpu
from jax.sharding import PartitionSpec as P

KVH = 8
HD = 128


EPS = 1e-05
THETA = 500000.0


def partner_2(value, axis, bit):
    mask = 2**bit
    pairs = [(source, source ^ mask) for source in range(lax.axis_size(axis))]
    return lax.ppermute(value, axis, pairs)


def rotary(tensor, positions):
    half_width = tensor.shape[-1] // 2
    frequency = THETA ** (-(jnp.arange(half_width, dtype=jnp.float32) * 2.0 / tensor.shape[-1]))
    angles = positions[:, None] * frequency[None, :]
    cosine = jnp.cos(angles)[:, None, :]
    sine_part = jnp.sin(angles)[:, None, :]
    first_half = tensor[..., :half_width]
    second_half = tensor[..., half_width:]
    return jnp.concatenate(
        (
            first_half * cosine - second_half * sine_part,
            second_half * cosine + first_half * sine_part,
        ),
        axis=-1,
    )


def rms_norm(hidden_in, norm_gain):
    wide = hidden_in.astype(jnp.float32)
    mean_square = jnp.mean(wide * wide, axis=-1, keepdims=True)
    return (wide * lax.rsqrt(mean_square + EPS) * norm_gain).astype(jnp.bfloat16)


def attend(queries, keys, values):
    length = queries.shape[1]
    scores = jnp.einsum(
        "bqhgd,bkhd->bhgqk", queries, keys, preferred_element_type=jnp.float32
    ) / math.sqrt(queries.shape[-1])
    causal = jnp.arange(length)[:, None] >= jnp.arange(length)[None, :]
    scores = jnp.where(causal, scores, -1e30)
    highest = jnp.max(scores, axis=-1, keepdims=True)
    exponent = jnp.exp(scores - highest)
    probabilities = (exponent / jnp.sum(exponent, axis=-1, keepdims=True)).astype(jnp.bfloat16)
    mixed = jnp.einsum(
        "bhgqk,bkhd->bqhgd", probabilities, values, preferred_element_type=jnp.float32
    )
    return mixed.astype(jnp.bfloat16)


def join_heads(stacked, axis_dim):
    sharers = max(lax.axis_size("tensor") // KVH, 1)
    position = lax.axis_index("tensor")
    for bit_index in range(sharers.bit_length() - 1):
        partner = partner_2(stacked, "tensor", bit_index)
        keeps_first = position // (1 << bit_index) % 2 == 0
        stacked = jnp.where(
            keeps_first,
            jnp.concatenate((stacked, partner), axis_dim),
            jnp.concatenate((partner, stacked), axis_dim),
        )
    return stacked


def general_shards(hidden_in, norm_gain, query_weight, kv_weight, output_weight):
    merged_weight = jnp.concatenate((query_weight, kv_weight), axis=1)
    query_cols = query_weight.shape[1]
    normed = rms_norm(hidden_in, norm_gain)
    projected = jnp.einsum(
        "brd,dc->brc",
        lax.all_gather(normed, "tensor", axis=0, tiled=True),
        merged_weight,
        preferred_element_type=jnp.float32,
    )
    batch, length = (projected.shape[0], projected.shape[1])
    queries_raw = projected[..., :query_cols]
    kv_raw = projected[..., query_cols:].astype(jnp.bfloat16)
    kv_raw = join_heads(kv_raw, 2)
    kv_heads = kv_raw.shape[-1] // (2 * HD)
    kv_split = kv_raw.reshape(batch, length, kv_heads, 2, HD)
    keys_raw = kv_split[:, :, :, 0, :]
    values = kv_split[:, :, :, 1, :]
    heads = query_cols // HD
    positions = jnp.arange(length, dtype=jnp.float32)
    queries = rotary(queries_raw.reshape(batch, length, heads, HD), positions).astype(jnp.bfloat16)
    keys = rotary(keys_raw.astype(jnp.float32), positions).astype(jnp.bfloat16)
    mixed = attend(queries.reshape(batch, length, kv_heads, heads // kv_heads, HD), keys, values)
    mixed_rows = mixed.reshape(batch, length, heads * HD)
    partial_out = jnp.einsum(
        "blc,cd->bld", mixed_rows, output_weight, preferred_element_type=jnp.float32
    )
    return lax.psum_scatter(
        partial_out.astype(jnp.bfloat16), "tensor", scatter_dimension=0, tiled=True
    )


MESH = pl.DeviceIdType.MESH
CORES = 2
HALVES = 2
LAG = 3
OUT_TILES = 8


def rotary_tables(length):
    half = HD // 2
    frequency = np.float32(THETA) ** (-(np.arange(half, dtype=np.float32) * np.float32(2.0 / HD)))
    angles = np.arange(length, dtype=np.float32)[:, None] * frequency[None, :].astype(np.float32)
    cosine, sine = np.cos(angles), np.sin(angles)
    return (
        np.concatenate((cosine, cosine), axis=1).astype(np.float32),
        np.concatenate((-sine, sine), axis=1).astype(np.float32),
    )


def block_kernel(
    dims,
    hid, gain_in, wq, wkv, wo, cosine_in, sine_in,
    out,
    gain, cosine, sine,
    x, xn, w1, w2, qs, ks, vs, mixed_own, mixed_far,
    give, got, held, summed, landed, own_acc, own_give, own_got,
    x_sem, w1_sem, w2_sem, sib_send, sib_recv, far_send, far_recv, fwd_send, fwd_recv,
    give_send, give_recv, sum_send, sum_recv, own_send, own_recv, table_sem,
):
    length, kvh, group, q_tiles, o_width = dims
    part = length // HALVES
    me = lax.axis_index("tensor")
    sibling = me + 1 - 2 * lax.rem(me, CORES)
    across = lax.rem(me + CORES, 2 * CORES)

    def local_copy(src, dst, sem):
        return pltpu.make_async_copy(src, dst, sem)

    def remote(src, dst, send, recv, target):
        return pltpu.make_async_remote_copy(
            src_ref=src, dst_ref=dst, send_sem=send, recv_sem=recv,
            device_id={"tensor": target}, device_id_type=MESH,
        )

    def w1_copy(t, kv):
        cols = pl.ds(pl.multiple_of(t * 2 * HD, 2 * HD), 2 * HD)
        if kv:
            return local_copy(wkv.at[:, cols], w1.at[t], w1_sem.at[t])
        return local_copy(wq.at[:, cols], w1.at[kvh + t], w1_sem.at[kvh + t])

    def w2_copy(j):
        cols = pl.ds(pl.multiple_of(j * o_width, o_width), o_width)
        return local_copy(wo.at[:, cols], w2.at[j], w2_sem.at[j])

    def far_copy(h):
        rows = pl.ds(h * part, part)
        return remote(hid.at[0, rows], x.at[2, rows], far_send.at[h], far_recv.at[h], across)

    def fwd_copy(h):
        rows = pl.ds(h * part, part)
        return remote(x.at[2, rows], x.at[3, rows], fwd_send.at[h], fwd_recv.at[h], sibling)

    def give_copy(h, j):
        return remote(give.at[h, j], got.at[h, j], give_send.at[h, j], give_recv.at[h, j], sibling)

    def sum_copy(h, j):
        return remote(summed.at[h, j], landed.at[h, j], sum_send.at[h, j], sum_recv.at[h, j], across)

    def own_copy(j):
        return remote(own_give.at[j], own_got.at[j], own_send.at[j], own_recv.at[j], sibling)

    x_copy = local_copy(hid.at[0], x.at[0], x_sem)
    sib_copy = remote(hid.at[0], x.at[1], sib_send, sib_recv, sibling)

    tables = [
        local_copy(src, dst, table_sem.at[i])
        for i, (src, dst) in enumerate(((gain_in, gain), (cosine_in, cosine), (sine_in, sine)))
    ]
    barrier = pltpu.get_barrier_semaphore()
    for target in (sibling, across):
        pl.semaphore_signal(barrier, inc=1, device_id={"tensor": target}, device_id_type=MESH)

    x_copy.start()
    for table in tables:
        table.start()
    for t in range(kvh):
        w1_copy(t, True).start()
    for t in range(q_tiles):
        w1_copy(t, False).start()
    for j in range(OUT_TILES):
        w2_copy(j).start()

    pl.semaphore_wait(barrier, 2)
    for h in range(HALVES):
        far_copy(h).start()
    sib_copy.start()

    def normalise(slot, row0, rows, dst0):
        step = 16

        def body(i, carry):
            at = pl.multiple_of(i * step, step)
            wide = x[slot, pl.ds(row0 + at, step), :].astype(jnp.float32)
            mean_square = jnp.mean(wide * wide, axis=-1, keepdims=True)
            scaled = wide * lax.rsqrt(mean_square + EPS) * gain[...]
            xn[pl.ds(dst0 + at, step), :] = scaled.astype(jnp.bfloat16)
            return carry

        lax.fori_loop(0, rows // step, body, 0)

    def rotate(value, row0, rows):
        c = cosine[row0 : row0 + rows, :]
        s = sine[row0 : row0 + rows, :]
        return value * c + pltpu.roll(value, HD // 2, 1) * s

    def project(slot0, row0, rows, first):
        both = 2 * rows

        def kv_body(g, carry):
            if first:
                w1_copy(g, True).wait()
            raw = jnp.dot(xn[:both, :], w1[g], preferred_element_type=jnp.float32).astype(jnp.bfloat16)
            for s in range(2):
                mine = raw[s * rows : (s + 1) * rows]
                keys = rotate(mine[:, :HD].astype(jnp.float32), row0, rows)
                ks[slot0 + s, g, row0 : row0 + rows, :] = keys.astype(jnp.bfloat16)
                vs[slot0 + s, g, row0 : row0 + rows, :] = mine[:, HD:]
            return carry

        def q_body(t, carry):
            if first:
                w1_copy(t, False).wait()
            raw = jnp.dot(xn[:both, :], w1[kvh + t], preferred_element_type=jnp.float32)
            for s in range(2):
                for e in range(2):
                    value = raw[s * rows : (s + 1) * rows, e * HD : (e + 1) * HD]
                    qs[s, 2 * t + e, :rows, :] = rotate(value, row0, rows).astype(jnp.bfloat16)
            return carry

        lax.fori_loop(0, kvh, kv_body, 0)
        lax.fori_loop(0, q_tiles, q_body, 0)

    def attention(slot0, row0, rows, mixed):
        seen = row0 + rows
        for s in range(2):
            for g in range(kvh):
                queries = qs[s, g * group : (g + 1) * group, :rows, :].reshape(group * rows, HD)
                keys = ks[slot0 + s, g, :seen, :]
                scores = lax.dot_general(
                    queries, keys, (((1,), (1,)), ((), ())), preferred_element_type=jnp.float32
                ) * (1.0 / math.sqrt(HD))
                scores = scores.reshape(group, rows, seen)
                position = row0 + lax.broadcasted_iota(jnp.int32, (group, rows, seen), 1)
                key_at = lax.broadcasted_iota(jnp.int32, (group, rows, seen), 2)
                scores = jnp.where(position >= key_at, scores, -1e30)
                highest = jnp.max(scores, axis=-1, keepdims=True)
                exponent = jnp.exp(scores - highest)
                total = jnp.sum(exponent, axis=-1, keepdims=True)
                probabilities = (exponent * (1.0 / total)).astype(jnp.bfloat16)
                result = jnp.dot(
                    probabilities.reshape(group * rows, seen),
                    vs[slot0 + s, g, :seen, :],
                    preferred_element_type=jnp.float32,
                ).astype(jnp.bfloat16)
                for e in range(group):
                    head = g * group + e
                    mixed[s * rows : (s + 1) * rows, head * HD : (head + 1) * HD] = result[
                        e * rows : (e + 1) * rows
                    ]

    for table in tables:
        table.wait()
    x_copy.wait()
    normalise(0, 0, length, 0)
    sib_copy.wait_recv()
    normalise(1, 0, length, length)
    project(0, 0, length, True)
    attention(0, 0, length, mixed_own)

    for h in range(HALVES):
        row0 = h * part
        far_copy(h).wait_recv()
        fwd_copy(h).start()
        normalise(2, row0, part, 0)
        fwd_copy(h).wait_recv()
        normalise(3, row0, part, part)
        project(2, row0, part, False)
        attention(2, row0, part, mixed_far)

        def far_out(j, carry, h=h):
            @pl.when(j < OUT_TILES)
            def _():
                if h == 0:
                    w2_copy(j).wait()
                partial = jnp.dot(mixed_far[...], w2[j], preferred_element_type=jnp.float32)
                held[j] = partial[:part]
                give[h, j] = partial[part:].astype(jnp.bfloat16)
                give_copy(h, j).start()

            @pl.when(j >= LAG)
            def _():
                t = j - LAG
                give_copy(h, t).wait_recv()
                summed[h, t] = (held[t] + got[h, t].astype(jnp.float32)).astype(jnp.bfloat16)
                sum_copy(h, t).start()

            return carry

        lax.fori_loop(0, OUT_TILES + LAG, far_out, 0)

    def own_out(j, carry):
        partial = jnp.dot(mixed_own[...], w2[j], preferred_element_type=jnp.float32)
        own_acc[j] = partial[:length]
        own_give[j] = partial[length:].astype(jnp.bfloat16)
        own_copy(j).start()
        return carry

    lax.fori_loop(0, OUT_TILES, own_out, 0)

    for h in range(HALVES):

        def finish(j, carry, h=h):
            rows = pl.ds(h * part, part)
            if h == 0:
                own_copy(j).wait_recv()
            sum_copy(h, j).wait_recv()
            cols = pl.ds(pl.multiple_of(j * o_width, o_width), o_width)
            out[0, rows, cols] = (
                own_acc[j, rows, :] + own_got[j, rows, :].astype(jnp.float32)
                + landed[h, j].astype(jnp.float32)
            ).astype(jnp.bfloat16)
            return carry

        lax.fori_loop(0, OUT_TILES, finish, 0)

    def drain(j, carry):
        own_copy(j).wait_send()
        for h in range(HALVES):
            give_copy(h, j).wait_send()
            sum_copy(h, j).wait_send()
        return carry

    lax.fori_loop(0, OUT_TILES, drain, 0)
    sib_copy.wait_send()
    for h in range(HALVES):
        far_copy(h).wait_send()
        fwd_copy(h).wait_send()


def paired_shards(hidden_in, norm_gain, query_weight, kv_weight, output_weight):
    _, length, width = hidden_in.shape
    query_cols, kv_cols = query_weight.shape[1], kv_weight.shape[1]
    heads, kvh = query_cols // HD, kv_cols // (2 * HD)
    q_tiles = query_cols // (2 * HD)
    part = length // HALVES
    o_width = width // OUT_TILES
    cosine, sine = rotary_tables(length)
    bf16, f32 = jnp.bfloat16, jnp.float32
    dma = pltpu.SemaphoreType.DMA
    any_spec = pl.BlockSpec(memory_space=pl.ANY)
    dims = (length, kvh, heads // kvh, q_tiles, o_width)
    return pl.pallas_call(
        functools.partial(block_kernel, dims),
        out_shape=pltpu.VMEM(hidden_in.shape, bf16),
        in_specs=[any_spec] * 7,
        out_specs=pl.BlockSpec(memory_space=pltpu.VMEM),
        scratch_shapes=[
            pltpu.VMEM((1, width), f32),
            pltpu.VMEM((length, HD), f32),
            pltpu.VMEM((length, HD), f32),
            pltpu.VMEM((4, length, width), bf16),
            pltpu.VMEM((2 * length, width), bf16),
            pltpu.VMEM((kvh + q_tiles, width, 2 * HD), bf16),
            pltpu.VMEM((OUT_TILES, query_cols, o_width), bf16),
            pltpu.VMEM((2, heads, length, HD), bf16),
            pltpu.VMEM((4, kvh, length, HD), bf16),
            pltpu.VMEM((4, kvh, length, HD), bf16),
            pltpu.VMEM((2 * length, query_cols), bf16),
            pltpu.VMEM((2 * part, query_cols), bf16),
            pltpu.VMEM((HALVES, OUT_TILES, part, o_width), bf16),
            pltpu.VMEM((HALVES, OUT_TILES, part, o_width), bf16),
            pltpu.VMEM((OUT_TILES, part, o_width), f32),
            pltpu.VMEM((HALVES, OUT_TILES, part, o_width), bf16),
            pltpu.VMEM((HALVES, OUT_TILES, part, o_width), bf16),
            pltpu.VMEM((OUT_TILES, length, o_width), f32),
            pltpu.VMEM((OUT_TILES, length, o_width), bf16),
            pltpu.VMEM((OUT_TILES, length, o_width), bf16),
            dma,
            dma((kvh + q_tiles,)),
            dma((OUT_TILES,)),
            dma, dma,
            dma((HALVES,)), dma((HALVES,)),
            dma((HALVES,)), dma((HALVES,)),
            dma((HALVES, OUT_TILES)), dma((HALVES, OUT_TILES)),
            dma((HALVES, OUT_TILES)), dma((HALVES, OUT_TILES)),
            dma((OUT_TILES,)), dma((OUT_TILES,)),
            dma((3,)),
        ],
        compiler_params=pltpu.CompilerParams(
            collective_id=0, has_side_effects=True, vmem_limit_bytes=60 * 2**20
        ),
    )(
        hidden_in, norm_gain.reshape(1, width), query_weight, kv_weight, output_weight,
        jnp.asarray(cosine), jnp.asarray(sine),
    )


def shards(hidden_in, norm_gain, query_weight, kv_weight, output_weight):
    two_chips = lax.axis_size("tensor") == 2 * CORES
    whole_heads = kv_weight.shape[1] % (2 * HD) == 0
    if two_chips and whole_heads and hidden_in.shape[0] == 1:
        return paired_shards(hidden_in, norm_gain, query_weight, kv_weight, output_weight)
    return general_shards(hidden_in, norm_gain, query_weight, kv_weight, output_weight)


def solution(mesh):
    placed = (
        P(("dp", "tensor"), None, None),
        P(),
        P(None, "tensor"),
        P(None, "tensor"),
        P("tensor", None),
    )
    return jax.shard_map(
        shards,
        mesh=mesh,
        in_specs=placed,
        out_specs=P(("dp", "tensor"), None, None),
        check_vma=False,
    )
```

profile of v0, /device:TPU:0, one launch (start us, length us, event | category | flops | bytes accessed | tf_op | source)
XLA Modules:
  0.0 51.6 jit_solution(12501634682836245916)
XLA Ops:
  0.0 50.6 %shard_map.73 = bf16[1,128,4096]{2,1,0:T(8,128)(2,1)S(1)} custom-call(bf16[1,128,4096]{2,1,0:T(8,128)(2,1)} %hid.1, f32[1,4096]{1,0:T(1,128)} %bitcast.1, bf16[4096,1024]{1,0:T(8,128)(2,1)} %wq.1, bf16[4096,512]{1,0:T(8,128)(2,1)} %wkv.1, bf16[1024,4096]{1,0:T(8,128)(2,1)} %wo.1, f32[128,128]{1,0:T(8,128)} %constant.4.clone.cosine_in, ...), custom_call_target="tpu_custom_call" | custom-call | tf_op jit(solution)/shard_map/pallas_call | solution.py:371
  50.6 1.0 %copy.9 = bf16[1,128,4096]{2,1,0:T(8,128)(2,1)} copy(bf16[1,128,4096]{2,1,0:T(8,128)(2,1)S(1)} %shard_map.73) | data formatting | bytes 2097152
where the time goes:
time: 51.7 us; the launch traced here: 51.6 us
  Pallas kernels  50.6 us (98%)
  local copies, waits for them, and re-layouts  0.97 us (2%)
    pallas_call x1, Pallas kernels, paired_shards(): pl.pallas_call(functools.partial(block_kernel, dims), out_shape=pltpu.VME...  50.6 us

commit v1 on v0

--- a/solution.py
+++ b/solution.py
@@ -111,8 +111,11 @@
 MESH = pl.DeviceIdType.MESH
 CORES = 2
 HALVES = 2
+PIECES = 2
 LAG = 3
 OUT_TILES = 8
+LAST_TILES = 1
+FIRST_ROWS = 16
 
 
 def rotary_tables(length):
@@ -120,30 +123,27 @@
     frequency = np.float32(THETA) ** (-(np.arange(half, dtype=np.float32) * np.float32(2.0 / HD)))
     angles = np.arange(length, dtype=np.float32)[:, None] * frequency[None, :].astype(np.float32)
     cosine, sine = np.cos(angles), np.sin(angles)
-    return (
-        np.concatenate((cosine, cosine), axis=1).astype(np.float32),
-        np.concatenate((-sine, sine), axis=1).astype(np.float32),
-    )
+    return np.stack(
+        (np.concatenate((cosine, cosine), axis=1), np.concatenate((-sine, sine), axis=1))
+    ).astype(np.float32)
 
 
 def block_kernel(
     dims,
-    hid, gain_in, wq, wkv, wo, cosine_in, sine_in,
+    hid, gain_in, wq_in, wkv_in, wo_in, table_in,
     out,
-    gain, cosine, sine,
-    x, xn, w1, w2, qs, ks, vs, mixed_own, mixed_far,
+    gain, table,
+    x, xn, wkv, wq, wo, qs, ks, vs, mixed_own, mixed_far,
     give, got, held, summed, landed, own_acc, own_give, own_got,
-    x_sem, w1_sem, w2_sem, sib_send, sib_recv, far_send, far_recv, fwd_send, fwd_recv,
-    give_send, give_recv, sum_send, sum_recv, own_send, own_recv, table_sem,
+    small_sem, w_sem, sib_sem, far_send, far_recv, fwd_send, fwd_recv,
+    give_send, give_recv, sum_send, sum_recv, own_sem,
 ):
     length, kvh, group, q_tiles, o_width = dims
     part = length // HALVES
+    piece = part // PIECES
     me = lax.axis_index("tensor")
     sibling = me + 1 - 2 * lax.rem(me, CORES)
     across = lax.rem(me + CORES, 2 * CORES)
-
-    def local_copy(src, dst, sem):
-        return pltpu.make_async_copy(src, dst, sem)
 
     def remote(src, dst, send, recv, target):
         return pltpu.make_async_remote_copy(
@@ -151,58 +151,56 @@
             device_id={"tensor": target}, device_id_type=MESH,
         )
 
-    def w1_copy(t, kv):
-        cols = pl.ds(pl.multiple_of(t * 2 * HD, 2 * HD), 2 * HD)
-        if kv:
-            return local_copy(wkv.at[:, cols], w1.at[t], w1_sem.at[t])
-        return local_copy(wq.at[:, cols], w1.at[kvh + t], w1_sem.at[kvh + t])
-
-    def w2_copy(j):
-        cols = pl.ds(pl.multiple_of(j * o_width, o_width), o_width)
-        return local_copy(wo.at[:, cols], w2.at[j], w2_sem.at[j])
-
-    def far_copy(h):
-        rows = pl.ds(h * part, part)
-        return remote(hid.at[0, rows], x.at[2, rows], far_send.at[h], far_recv.at[h], across)
-
-    def fwd_copy(h):
-        rows = pl.ds(h * part, part)
-        return remote(x.at[2, rows], x.at[3, rows], fwd_send.at[h], fwd_recv.at[h], sibling)
+    q_cols = q_tiles * HD
+    kv_copy = pltpu.make_async_copy(wkv_in, wkv, w_sem.at[0])
+    q_copies = [
+        pltpu.make_async_copy(
+            wq_in.at[:, pl.ds(i * q_cols, q_cols)], wq.at[:, pl.ds(i * q_cols, q_cols)], w_sem.at[1 + i]
+        )
+        for i in range(2)
+    ]
+    o_copy = pltpu.make_async_copy(wo_in, wo, w_sem.at[3])
+    x_copy = pltpu.make_async_copy(hid.at[0], x.at[0], small_sem.at[0])
+    gain_copy = pltpu.make_async_copy(gain_in, gain, small_sem.at[1])
+    table_copy = pltpu.make_async_copy(table_in, table, small_sem.at[2])
+    sib_copy = remote(x.at[0], x.at[1], sib_sem.at[0], sib_sem.at[1], sibling)
+
+    def far_copy(src, row0, rows, p):
+        at = pl.ds(row0, rows)
+        return remote(src.at[0, at], x.at[2, at], far_send, far_recv.at[p], across)
+
+    def fwd_copy(row0, rows, p):
+        at = pl.ds(row0, rows)
+        return remote(x.at[2, at], x.at[3, at], fwd_send, fwd_recv.at[p], sibling)
 
     def give_copy(h, j):
-        return remote(give.at[h, j], got.at[h, j], give_send.at[h, j], give_recv.at[h, j], sibling)
-
-    def sum_copy(h, j):
-        return remote(summed.at[h, j], landed.at[h, j], sum_send.at[h, j], sum_recv.at[h, j], across)
-
-    def own_copy(j):
-        return remote(own_give.at[j], own_got.at[j], own_send.at[j], own_recv.at[j], sibling)
-
-    x_copy = local_copy(hid.at[0], x.at[0], x_sem)
-    sib_copy = remote(hid.at[0], x.at[1], sib_send, sib_recv, sibling)
-
-    tables = [
-        local_copy(src, dst, table_sem.at[i])
-        for i, (src, dst) in enumerate(((gain_in, gain), (cosine_in, cosine), (sine_in, sine)))
-    ]
+        return remote(give.at[h, j], got.at[h, j], give_send, give_recv.at[j], sibling)
+
+    def sum_copy(h, j, count, i):
+        at = pl.ds(j, count)
+        return remote(summed.at[h, at], landed.at[h, at], sum_send, sum_recv.at[i], across)
+
+    def own_copy(j, count):
+        at = pl.ds(j, count)
+        return remote(own_give.at[at], own_got.at[at], own_sem.at[0], own_sem.at[1], sibling)
+
     barrier = pltpu.get_barrier_semaphore()
-    for target in (sibling, across):
+    for target in (across, sibling):
         pl.semaphore_signal(barrier, inc=1, device_id={"tensor": target}, device_id_type=MESH)
-
     x_copy.start()
-    for table in tables:
-        table.start()
-    for t in range(kvh):
-        w1_copy(t, True).start()
-    for t in range(q_tiles):
-        w1_copy(t, False).start()
-    for j in range(OUT_TILES):
-        w2_copy(j).start()
-
+    gain_copy.start()
+    table_copy.start()
     pl.semaphore_wait(barrier, 2)
-    for h in range(HALVES):
-        far_copy(h).start()
+    far_copy(hid, 0, FIRST_ROWS, 0).start()
+    x_copy.wait()
+    far_copy(x, FIRST_ROWS, piece - FIRST_ROWS, 0).start()
+    for p in range(1, HALVES * PIECES):
+        far_copy(x, p * piece, piece, p).start()
     sib_copy.start()
+    kv_copy.start()
+    for q_copy in q_copies:
+        q_copy.start()
+    o_copy.start()
 
     def normalise(slot, row0, rows, dst0):
         step = 16
@@ -218,17 +216,20 @@
         lax.fori_loop(0, rows // step, body, 0)
 
     def rotate(value, row0, rows):
-        c = cosine[row0 : row0 + rows, :]
-        s = sine[row0 : row0 + rows, :]
+        c = table[0, row0 : row0 + rows, :]
+        s = table[1, row0 : row0 + rows, :]
         return value * c + pltpu.roll(value, HD // 2, 1) * s
+
+    def columns(t, width):
+        return pl.ds(pl.multiple_of(t * width, width), width)
 
     def project(slot0, row0, rows, first):
         both = 2 * rows
 
         def kv_body(g, carry):
-            if first:
-                w1_copy(g, True).wait()
-            raw = jnp.dot(xn[:both, :], w1[g], preferred_element_type=jnp.float32).astype(jnp.bfloat16)
+            raw = jnp.dot(
+                xn[:both, :], wkv[:, columns(g, 2 * HD)], preferred_element_type=jnp.float32
+            ).astype(jnp.bfloat16)
             for s in range(2):
                 mine = raw[s * rows : (s + 1) * rows]
                 keys = rotate(mine[:, :HD].astype(jnp.float32), row0, rows)
@@ -237,17 +238,22 @@
             return carry
 
         def q_body(t, carry):
-            if first:
-                w1_copy(t, False).wait()
-            raw = jnp.dot(xn[:both, :], w1[kvh + t], preferred_element_type=jnp.float32)
+            raw = jnp.dot(xn[:both, :], wq[:, columns(t, 2 * HD)], preferred_element_type=jnp.float32)
             for s in range(2):
                 for e in range(2):
                     value = raw[s * rows : (s + 1) * rows, e * HD : (e + 1) * HD]
                     qs[s, 2 * t + e, :rows, :] = rotate(value, row0, rows).astype(jnp.bfloat16)
             return carry
 
+        if first:
+            kv_copy.wait()
         lax.fori_loop(0, kvh, kv_body, 0)
-        lax.fori_loop(0, q_tiles, q_body, 0)
+        if first:
+            for i in range(2):
+                q_copies[i].wait()
+                lax.fori_loop(i * q_tiles // 2, (i + 1) * q_tiles // 2, q_body, 0)
+        else:
+            lax.fori_loop(0, q_tiles, q_body, 0)
 
     def attention(slot0, row0, rows, mixed):
         seen = row0 + rows
@@ -277,31 +283,46 @@
                         e * rows : (e + 1) * rows
                     ]
 
-    for table in tables:
-        table.wait()
-    x_copy.wait()
+    gain_copy.wait()
+    table_copy.wait()
     normalise(0, 0, length, 0)
     sib_copy.wait_recv()
     normalise(1, 0, length, length)
     project(0, 0, length, True)
     attention(0, 0, length, mixed_own)
 
+    def own_out(j, carry):
+        partial = jnp.dot(
+            mixed_own[...], wo[:, columns(j, o_width)], preferred_element_type=jnp.float32
+        )
+        own_acc[j] = partial[:length]
+        own_give[j] = partial[length:].astype(jnp.bfloat16)
+        own_copy(j, 1).start()
+        return carry
+
+    o_copy.wait()
+    lax.fori_loop(0, OUT_TILES, own_out, 0)
+
     for h in range(HALVES):
         row0 = h * part
-        far_copy(h).wait_recv()
-        fwd_copy(h).start()
-        normalise(2, row0, part, 0)
-        fwd_copy(h).wait_recv()
-        normalise(3, row0, part, part)
+        for p in range(PIECES):
+            at = p * piece
+            far_copy(x, row0 + at, piece, h * PIECES + p).wait_recv()
+            fwd_copy(row0 + at, piece, h * PIECES + p).start()
+            normalise(2, row0 + at, piece, at)
+        for p in range(PIECES):
+            at = p * piece
+            fwd_copy(row0 + at, piece, h * PIECES + p).wait_recv()
+            normalise(3, row0 + at, piece, part + at)
         project(2, row0, part, False)
         attention(2, row0, part, mixed_far)
 
         def far_out(j, carry, h=h):
             @pl.when(j < OUT_TILES)
             def _():
-                if h == 0:
-                    w2_copy(j).wait()
-                partial = jnp.dot(mixed_far[...], w2[j], preferred_element_type=jnp.float32)
+                partial = jnp.dot(
+                    mixed_far[...], wo[:, columns(j, o_width)], preferred_element_type=jnp.float32
+                )
                 held[j] = partial[:part]
                 give[h, j] = partial[part:].astype(jnp.bfloat16)
                 give_copy(h, j).start()
@@ -311,49 +332,44 @@
                 t = j - LAG
                 give_copy(h, t).wait_recv()
                 summed[h, t] = (held[t] + got[h, t].astype(jnp.float32)).astype(jnp.bfloat16)
-                sum_copy(h, t).start()
+                if h < HALVES - 1:
+                    sum_copy(h, t, 1, h).start()
+                else:
+                    late = (t >= OUT_TILES - LAST_TILES).astype(jnp.int32)
+                    sum_copy(h, t, 1, h + late).start()
 
             return carry
 
         lax.fori_loop(0, OUT_TILES + LAG, far_out, 0)
 
-    def own_out(j, carry):
-        partial = jnp.dot(mixed_own[...], w2[j], preferred_element_type=jnp.float32)
-        own_acc[j] = partial[:length]
-        own_give[j] = partial[length:].astype(jnp.bfloat16)
-        own_copy(j).start()
+    own_copy(0, OUT_TILES).wait_recv()
+
+    def join(j, carry):
+        own_acc[j] = own_acc[j] + own_got[j].astype(jnp.float32)
         return carry
 
-    lax.fori_loop(0, OUT_TILES, own_out, 0)
-
-    for h in range(HALVES):
+    lax.fori_loop(0, OUT_TILES, join, 0)
+
+    spans = [(h, 0, OUT_TILES) for h in range(HALVES - 1)]
+    spans += [(HALVES - 1, 0, OUT_TILES - LAST_TILES), (HALVES - 1, OUT_TILES - LAST_TILES, LAST_TILES)]
+    for i, (h, j0, count) in enumerate(spans):
 
         def finish(j, carry, h=h):
             rows = pl.ds(h * part, part)
-            if h == 0:
-                own_copy(j).wait_recv()
-            sum_copy(h, j).wait_recv()
-            cols = pl.ds(pl.multiple_of(j * o_width, o_width), o_width)
-            out[0, rows, cols] = (
-                own_acc[j, rows, :] + own_got[j, rows, :].astype(jnp.float32)
-                + landed[h, j].astype(jnp.float32)
+            out[0, rows, columns(j, o_width)] = (
+                own_acc[j, rows, :] + landed[h, j].astype(jnp.float32)
             ).astype(jnp.bfloat16)
             return carry
 
-        lax.fori_loop(0, OUT_TILES, finish, 0)
-
-    def drain(j, carry):
-        own_copy(j).wait_send()
-        for h in range(HALVES):
-            give_copy(h, j).wait_send()
-            sum_copy(h, j).wait_send()
-        return carry
-
-    lax.fori_loop(0, OUT_TILES, drain, 0)
+        sum_copy(h, j0, count, i).wait_recv()
+        lax.fori_loop(j0, j0 + count, finish, 0)
+
+    own_copy(0, OUT_TILES).wait_send()
+    remote(give, got, give_send, give_recv.at[0], sibling).wait_send()
+    remote(summed, landed, sum_send, sum_recv.at[0], across).wait_send()
     sib_copy.wait_send()
-    for h in range(HALVES):
-        far_copy(h).wait_send()
-        fwd_copy(h).wait_send()
+    far_copy(x, 0, length, 0).wait_send()
+    fwd_copy(0, length, 0).wait_send()
 
 
 def paired_shards(hidden_in, norm_gain, query_weight, kv_weight, output_weight):
@@ -363,7 +379,6 @@
     q_tiles = query_cols // (2 * HD)
     part = length // HALVES
     o_width = width // OUT_TILES
-    cosine, sine = rotary_tables(length)
     bf16, f32 = jnp.bfloat16, jnp.float32
     dma = pltpu.SemaphoreType.DMA
     any_spec = pl.BlockSpec(memory_space=pl.ANY)
@@ -371,16 +386,16 @@
     return pl.pallas_call(
         functools.partial(block_kernel, dims),
         out_shape=pltpu.VMEM(hidden_in.shape, bf16),
-        in_specs=[any_spec] * 7,
+        in_specs=[any_spec] * 6,
         out_specs=pl.BlockSpec(memory_space=pltpu.VMEM),
         scratch_shapes=[
             pltpu.VMEM((1, width), f32),
-            pltpu.VMEM((length, HD), f32),
-            pltpu.VMEM((length, HD), f32),
+            pltpu.VMEM((2, length, HD), f32),
             pltpu.VMEM((4, length, width), bf16),
             pltpu.VMEM((2 * length, width), bf16),
-            pltpu.VMEM((kvh + q_tiles, width, 2 * HD), bf16),
-            pltpu.VMEM((OUT_TILES, query_cols, o_width), bf16),
+            pltpu.VMEM((width, kv_cols), bf16),
+            pltpu.VMEM((width, query_cols), bf16),
+            pltpu.VMEM((query_cols, width), bf16),
             pltpu.VMEM((2, heads, length, HD), bf16),
             pltpu.VMEM((4, kvh, length, HD), bf16),
             pltpu.VMEM((4, kvh, length, HD), bf16),
@@ -394,23 +409,21 @@
             pltpu.VMEM((OUT_TILES, length, o_width), f32),
             pltpu.VMEM((OUT_TILES, length, o_width), bf16),
             pltpu.VMEM((OUT_TILES, length, o_width), bf16),
-            dma,
-            dma((kvh + q_tiles,)),
-            dma((OUT_TILES,)),
-            dma, dma,
-            dma((HALVES,)), dma((HALVES,)),
-            dma((HALVES,)), dma((HALVES,)),
-            dma((HALVES, OUT_TILES)), dma((HALVES, OUT_TILES)),
-            dma((HALVES, OUT_TILES)), dma((HALVES, OUT_TILES)),
-            dma((OUT_TILES,)), dma((OUT_TILES,)),
             dma((3,)),
+            dma((4,)),
+            dma((2,)),
+            dma, dma((HALVES * PIECES,)),
+            dma, dma((HALVES * PIECES,)),
+            dma, dma((OUT_TILES,)),
+            dma, dma((HALVES + 1,)),
+            dma((2,)),
         ],
         compiler_params=pltpu.CompilerParams(
             collective_id=0, has_side_effects=True, vmem_limit_bytes=60 * 2**20
         ),
     )(
         hidden_in, norm_gain.reshape(1, width), query_weight, kv_weight, output_weight,
-        jnp.asarray(cosine), jnp.asarray(sine),
+        jnp.asarray(rotary_tables(length)),
     )
 
 

time: 51.7 us -> 51 us (0.986)
  Pallas kernels: 50.6 us -> 49.8 us
    pallas_call x1, Pallas kernels: 50.6 us -> 49.8 us  [paired_shards(): pl.pallas_call(functools.partial(block_kernel, dims), out_shape=pltpu.VME...]
where the time goes in v1:
time: 51 us; the launch traced here: 50.8 us
  Pallas kernels  49.8 us (98%)
  local copies, waits for them, and re-layouts  0.97 us (2%)
    pallas_call x1, Pallas kernels, paired_shards(): pl.pallas_call(functools.partial(block_kernel, dims), out_shape=pltpu.VME...  49.8 us

profile of v1, /device:TPU:0, one launch (start us, length us, event | category | flops | bytes accessed | tf_op | source)
XLA Modules:
  0.0 50.8 jit_solution(1420883973209387479)
XLA Ops:
  0.0 49.8 %shard_map.64 = bf16[1,128,4096]{2,1,0:T(8,128)(2,1)S(1)} custom-call(bf16[1,128,4096]{2,1,0:T(8,128)(2,1)} %hid.1, f32[1,4096]{1,0:T(1,128)} %bitcast.1, bf16[4096,1024]{1,0:T(8,128)(2,1)} %wq_in.1, bf16[4096,512]{1,0:T(8,128)(2,1)} %wkv_in.1, bf16[1024,4096]{1,0:T(8,128)(2,1)} %wo_in.1, f32[2,128,128]{2,1,0:T(8,128)} %constant.2.clone.table_in), custom_call_target="tpu_custom_call" | custom-call | tf_op jit(solution)/shard_map/pallas_call | solution.py:386
  49.8 1.0 %copy.8 = bf16[1,128,4096]{2,1,0:T(8,128)(2,1)} copy(bf16[1,128,4096]{2,1,0:T(8,128)(2,1)S(1)} %shard_map.64) | data formatting | bytes 2097152

commit v2 on v1

--- a/solution.py
+++ b/solution.py
@@ -116,6 +116,8 @@
 OUT_TILES = 8
 LAST_TILES = 1
 FIRST_ROWS = 16
+RELAYS = (1, 2, 3, 4)
+RELAY_TILE = 0
 
 
 def rotary_tables(length):
@@ -136,7 +138,7 @@
     x, xn, wkv, wq, wo, qs, ks, vs, mixed_own, mixed_far,
     give, got, held, summed, landed, own_acc, own_give, own_got,
     small_sem, w_sem, sib_sem, far_send, far_recv, fwd_send, fwd_recv,
-    give_send, give_recv, sum_send, sum_recv, own_sem,
+    give_send, give_recv, sum_send, sum_recv, own_sem, relay, relay_sem, relay_ready,
 ):
     length, kvh, group, q_tiles, o_width = dims
     part = length // HALVES
@@ -144,6 +146,12 @@
     me = lax.axis_index("tensor")
     sibling = me + 1 - 2 * lax.rem(me, CORES)
     across = lax.rem(me + CORES, 2 * CORES)
+    group_at = lax.axis_index("dp")
+    relays = [r for r in RELAYS if r < lax.axis_size("dp")]
+    relay_rows = part // max(len(relays), 1)
+    is_target = (group_at == 0) & (me == 0)
+    is_source = (group_at == 0) & (me == CORES)
+    forwards = [(group_at == r) & (me == 0) for r in relays]
 
     def remote(src, dst, send, recv, target):
         return pltpu.make_async_remote_copy(
@@ -180,6 +188,20 @@
         at = pl.ds(j, count)
         return remote(summed.at[h, at], landed.at[h, at], sum_send, sum_recv.at[i], across)
 
+    def relay_copy(i):
+        at = pl.ds(i * relay_rows, relay_rows)
+        return pltpu.make_async_remote_copy(
+            src_ref=summed.at[HALVES - 1, RELAY_TILE, at], dst_ref=relay, send_sem=sum_send,
+            recv_sem=relay_sem.at[0], device_id={"dp": relays[i], "tensor": 0}, device_id_type=MESH,
+        )
+
+    def forward_copy(i):
+        at = pl.ds(i * relay_rows, relay_rows)
+        return pltpu.make_async_remote_copy(
+            src_ref=relay, dst_ref=landed.at[HALVES - 1, RELAY_TILE, at], send_sem=relay_sem.at[1],
+            recv_sem=sum_recv.at[HALVES - 1], device_id={"dp": 0, "tensor": 0}, device_id_type=MESH,
+        )
+
     def own_copy(j, count):
         at = pl.ds(j, count)
         return remote(own_give.at[at], own_got.at[at], own_sem.at[0], own_sem.at[1], sibling)
@@ -187,10 +209,27 @@
     barrier = pltpu.get_barrier_semaphore()
     for target in (across, sibling):
         pl.semaphore_signal(barrier, inc=1, device_id={"tensor": target}, device_id_type=MESH)
+    for r in relays:
+
+        @pl.when(is_target | is_source)
+        def _(r=r):
+            pl.semaphore_signal(
+                barrier, inc=1, device_id={"dp": r, "tensor": 0}, device_id_type=MESH
+            )
+
     x_copy.start()
     gain_copy.start()
     table_copy.start()
-    pl.semaphore_wait(barrier, 2)
+    peers = 2 + sum(2 * forwarding.astype(jnp.int32) for forwarding in forwards)
+    pl.semaphore_wait(barrier, peers)
+    for forwarding in forwards:
+
+        @pl.when(forwarding)
+        def _():
+            pl.semaphore_signal(
+                relay_ready, inc=1, device_id={"dp": 0, "tensor": CORES}, device_id_type=MESH
+            )
+
     far_copy(hid, 0, FIRST_ROWS, 0).start()
     x_copy.wait()
     far_copy(x, FIRST_ROWS, piece - FIRST_ROWS, 0).start()
@@ -336,7 +375,17 @@
                     sum_copy(h, t, 1, h).start()
                 else:
                     late = (t >= OUT_TILES - LAST_TILES).astype(jnp.int32)
-                    sum_copy(h, t, 1, h + late).start()
+                    relayed = is_source & (t == RELAY_TILE) & (len(relays) > 0)
+
+                    @pl.when(relayed)
+                    def _():
+                        pl.semaphore_wait(relay_ready, len(relays))
+                        for i in range(len(relays)):
+                            relay_copy(i).start()
+
+                    @pl.when(jnp.logical_not(relayed))
+                    def _():
+                        sum_copy(h, t, 1, h + late).start()
 
             return carry
 
@@ -349,6 +398,13 @@
         return carry
 
     lax.fori_loop(0, OUT_TILES, join, 0)
+    for i, forwarding in enumerate(forwards):
+
+        @pl.when(forwarding)
+        def _(i=i):
+            relay_copy(i).wait_recv()
+            forward_copy(i).start()
+
 
     spans = [(h, 0, OUT_TILES) for h in range(HALVES - 1)]
     spans += [(HALVES - 1, 0, OUT_TILES - LAST_TILES), (HALVES - 1, OUT_TILES - LAST_TILES, LAST_TILES)]
@@ -363,6 +419,12 @@
 
         sum_copy(h, j0, count, i).wait_recv()
         lax.fori_loop(j0, j0 + count, finish, 0)
+
+    for i, forwarding in enumerate(forwards):
+
+        @pl.when(forwarding)
+        def _(i=i):
+            forward_copy(i).wait_send()
 
     own_copy(0, OUT_TILES).wait_send()
     remote(give, got, give_send, give_recv.at[0], sibling).wait_send()
@@ -379,6 +441,7 @@
     q_tiles = query_cols // (2 * HD)
     part = length // HALVES
     o_width = width // OUT_TILES
+    relays = len([r for r in RELAYS if r < lax.axis_size("dp")])
     bf16, f32 = jnp.bfloat16, jnp.float32
     dma = pltpu.SemaphoreType.DMA
     any_spec = pl.BlockSpec(memory_space=pl.ANY)
@@ -417,6 +480,9 @@
             dma, dma((OUT_TILES,)),
             dma, dma((HALVES + 1,)),
             dma((2,)),
+            pltpu.VMEM((part // max(relays, 1), o_width), bf16),
+            dma((2,)),
+            pltpu.SemaphoreType.REGULAR,
         ],
         compiler_params=pltpu.CompilerParams(
             collective_id=0, has_side_effects=True, vmem_limit_bytes=60 * 2**20

time: 51 us -> 49.8 us (0.976)
  Pallas kernels: 49.8 us -> 48.7 us
    pallas_call x1, Pallas kernels: 49.8 us -> 48.7 us  [paired_shards(): pl.pallas_call(functools.partial(block_kernel, dims), out_shape=pltpu.VME...]
where the time goes in v2:
time: 49.8 us; the launch traced here: 49.7 us
  Pallas kernels  48.7 us (98%)
  local copies, waits for them, and re-layouts  0.97 us (2%)
    pallas_call x1, Pallas kernels, paired_shards(): pl.pallas_call(functools.partial(block_kernel, dims), out_shape=pltpu.VME...  48.7 us

profile of v2, /device:TPU:0, one launch (start us, length us, event | category | flops | bytes accessed | tf_op | source)
XLA Modules:
  0.0 49.7 jit_solution(14249733249513248269)
XLA Ops:
  0.0 48.7 %shard_map.64 = bf16[1,128,4096]{2,1,0:T(8,128)(2,1)S(1)} custom-call(bf16[1,128,4096]{2,1,0:T(8,128)(2,1)} %hid.1, f32[1,4096]{1,0:T(1,128)} %bitcast.1, bf16[4096,1024]{1,0:T(8,128)(2,1)} %wq_in.1, bf16[4096,512]{1,0:T(8,128)(2,1)} %wkv_in.1, bf16[1024,4096]{1,0:T(8,128)(2,1)} %wo_in.1, f32[2,128,128]{2,1,0:T(8,128)} %constant.2.clone.table_in), custom_call_target="tpu_custom_call" | custom-call | tf_op jit(solution)/shard_map/pallas_call | solution.py:449
  48.7 1.0 %copy.8 = bf16[1,128,4096]{2,1,0:T(8,128)(2,1)} copy(bf16[1,128,4096]{2,1,0:T(8,128)(2,1)S(1)} %shard_map.64) | data formatting | bytes 2097152
